TPU v7x, 512 devices: a whole 4x8x8 slice. The times are simulated.
512 devices in a mesh: section: 4 (over x_hi, core), seq: 128 (over z, y, x_lo).
Axes of the slice: x: 4 (x_hi: 2, x_lo: 2; x = x_hi * 2 + x_lo), y: 8, z: 8, core: 2. Of those that a mesh axis runs over, the one named last changes fastest.
Arguments:
- hidden: bfloat16 [2, 16384, 2688], P(None, 'seq'), may hold values from -6 to 6
- lengths: int32 [2], replicated, may hold values from 8192 to 16384, as said below
- reward_pos: int32 [2], replicated, may hold values from 8064 to 16383, as said below
- in_gain: bfloat16 [2688], P('seq'), may hold values from 0.099609375 to 1.8984375
- w_query: bfloat16 [2688, 2048], P('seq', 'section'), may hold values from -0.077151675 to 0.077151675
- w_key: bfloat16 [2688, 1024], P('seq', 'section'), may hold values from -0.077151675 to 0.077151675
- w_value: bfloat16 [2688, 1024], P('seq', 'section'), may hold values from -0.125 to 0.125
- query_gain: float32 [128], replicated, may hold values from 0.6 to 7
- key_gain: float32 [128], replicated, may hold values from 0.6 to 7
- w_out: bfloat16 [2048, 2688], P('section', 'seq'), may hold values from -0.125 to 0.125
- post_gain: bfloat16 [2688], P('seq'), may hold values from 0.099609375 to 1.8984375
- final_gain: bfloat16 [2688], P('seq'), may hold values from 0.099609375 to 1.8984375
- value_head: bfloat16 [2688], P('seq'), may hold values from -0.125 to 0.125
Outputs:
- token_values: float32 [2, 16384], P(None, 'seq')
- reward: float32 [2], replicated
Inputs may be any that keep to these rules, and one draw needn't show every extreme that they name: `lengths`: in every draw at least one micro-batch has all 16384 tokens valid. reward_pos[m] lies among the last 128 valid tokens of micro-batch m.
All inputs are finite; a program needn't handle non-finite values.
Results may differ from a plain program's by a relative error of at most 0.01.
Values may be sent and summed in bfloat16 or wider, within the bound.
No kernel may reach another device: no remote copies, remote signals or barrier semaphores. Data moves between devices by JAX's collectives and lax.ppermute only.
A program may use at most 64 MiB of HBM per device.

v0:
```python
import functools
import math
import jax
import jax.numpy as jnp
from jax import lax
from jax.sharding import Mesh
from jax.sharding import PartitionSpec as P

HD = 128
GROUP = 2
WINDOW = 1024
SEQ = ("seq_0", "seq_1", "seq_2")
norm_eps = 1e-06
query_scale = 168.0 ** (-0.5)
rope_base = 10000.0


def passed_along(array, axis, by):
    devices = lax.axis_size(axis)
    pairs = [(i, i + by) for i in range(devices) if 0 <= i + by < devices]
    return lax.ppermute(array, axis, pairs)


def sent_together(arrays, axis, dim, along):
    widths = [math.prod(a.shape[along:]) for a in arrays]
    both = jnp.concatenate(
        [a.reshape(*a.shape[:along], w) for a, w in zip(arrays, widths)], axis=along
    )
    whole = lax.all_gather(both, axis, axis=dim, tiled=True)
    tiles = jnp.split(whole, [sum(widths[:k]) for k in range(1, len(widths))], axis=along)
    return tuple((b.reshape(*whole.shape[:along], *a.shape[along:]) for a, b in zip(arrays, tiles)))


def laid_out(tiles, dim):
    tiles = jnp.moveaxis(tiles, 0, dim)
    lengths = tiles.shape
    return tiles.reshape(*lengths[:dim], lengths[dim] * lengths[dim + 1], *lengths[dim + 2 :])


def stacked_from(array, axes, turns):
    tiles = array[None]
    for k in turns:
        tiles = lax.all_gather(tiles, axes[k], axis=0, tiled=True)
    held = [lax.axis_size(axes[k]) for k in reversed(turns)]
    tiles = tiles.reshape(*held, *array.shape)
    turned = sorted(range(len(turns)), key=lambda place: turns[len(turns) - 1 - place])
    return tiles.transpose(*turned, *range(len(turns), tiles.ndim)).reshape(-1, *array.shape)


def whole_of(array, axes, turns, dim):
    return laid_out(stacked_from(array, axes, turns), dim)


def in_blocks(array, dim, devices):
    before, after = (array.shape[:dim], array.shape[dim + 1 :])
    return jnp.moveaxis(array.reshape(*before, devices, -1, *after), dim, 0)


def sent_and_summed(array, axis, dim):
    tiles = in_blocks(array, dim, lax.axis_size(axis))
    arrived = lax.all_to_all(tiles, axis, split_axis=0, concat_axis=0, tiled=True)
    return arrived.sum(axis=0)


def sent_to_all(array, axis):
    devices = lax.axis_size(axis)
    return lax.all_to_all(
        jnp.broadcast_to(array[None], (devices, *array.shape)), axis, 0, 0, tiled=True
    )


def taken_together(array, axis):
    everything = sent_to_all(array, axis)
    return jnp.sum(everything, axis=0)


def by_axis(array, axes):
    return functools.reduce(lax.psum, axes, array)


def rms_scale(values, gain_vec):
    return (
        values * lax.rsqrt(jnp.mean(values * values, axis=-1, keepdims=True) + norm_eps) * gain_vec
    )


def rotate_pairs(head_rows, positions):
    half_width = head_rows.shape[-1] // 2
    frequency = rope_base ** (
        -jnp.arange(half_width, dtype=jnp.float32) * 2.0 / head_rows.shape[-1]
    )
    angles = positions.astype(jnp.float32)[:, None] * frequency[None, :]
    target = (angles.shape[0],) + (1,) * (head_rows.ndim - 2) + (half_width,)
    cosine = jnp.cos(angles).reshape(target)
    sine_part = jnp.sin(angles).reshape(target)
    front_half = head_rows[..., :half_width]
    back_half = head_rows[..., half_width:]
    return jnp.concatenate(
        [front_half * cosine - back_half * sine_part, back_half * cosine + front_half * sine_part],
        axis=-1,
    )


def window_blocks(packed, tok_dev):
    block_count = WINDOW // tok_dev + 1
    blocks_held = [packed]
    while len(blocks_held) < block_count:
        take_count = min(len(blocks_held), block_count - len(blocks_held))
        arrived = passed_along(jnp.stack(blocks_held[:take_count]), SEQ, len(blocks_held))
        blocks_held = blocks_held + [arrived[offset] for offset in range(take_count)]
    return jnp.concatenate(blocks_held[::-1], axis=1)


def window_attention(queries, keys_all, values_all, query_pos, key_pos):
    scores = jnp.einsum("qhgd,khd->hgqk", queries, keys_all, preferred_element_type=jnp.float32)
    allowed = (
        (key_pos[None, :] <= query_pos[:, None])
        & (key_pos[None, :] > query_pos[:, None] - WINDOW)
        & (key_pos[None, :] >= 0)
    )
    scores = jnp.where(allowed[None, None], scores, -1e30)
    row_top = jnp.max(scores, axis=-1, keepdims=True)
    exponent = jnp.exp(scores - row_top)
    attn_weights = (exponent / jnp.sum(exponent, axis=-1, keepdims=True)).astype(jnp.bfloat16)
    mixed_heads = jnp.einsum(
        "hgqk,khd->qhgd", attn_weights, values_all, preferred_element_type=jnp.float32
    )
    return mixed_heads.astype(jnp.bfloat16)


def local(
    hidden,
    lengths,
    reward_pos,
    in_gain,
    w_query,
    w_key,
    w_value,
    query_gain,
    key_gain,
    w_out,
    post_gain,
    final_gain,
    value_head,
):
    micro_count, tok_dev, width = hidden.shape
    row_count = micro_count * tok_dev
    qwidth = w_query.shape[1]
    kwidth = w_key.shape[1]
    heads_here = kwidth // HD
    widened = hidden.reshape(row_count, width).astype(jnp.float32)
    inverse = lax.rsqrt(jnp.mean(widened * widened, axis=-1, keepdims=True) + norm_eps)
    seq_pos = lax.axis_index(SEQ) * tok_dev + jnp.arange(tok_dev, dtype=jnp.int32)
    positions = jnp.tile(seq_pos, micro_count)
    gain_piece, query_piece, key_piece, value_piece, post_piece, final_piece, head_piece = (
        sent_together(
            (in_gain, w_query, w_key, w_value, post_gain, final_gain, value_head), SEQ, 0, 1
        )
    )
    normed = (widened * inverse * gain_piece.astype(jnp.float32)).astype(jnp.bfloat16)
    query_acc = jnp.dot(normed, query_piece, preferred_element_type=jnp.float32)
    key_acc = jnp.dot(normed, key_piece, preferred_element_type=jnp.float32)
    value_acc = jnp.dot(normed, value_piece, preferred_element_type=jnp.float32)
    post_full = post_piece.astype(jnp.float32)
    final_full = final_piece.astype(jnp.float32)
    head_full = head_piece.astype(jnp.float32)
    folded = (query_acc, key_acc, value_acc, post_full, final_full, head_full)
    queries = folded[0].reshape(row_count, heads_here, GROUP, HD)
    queries = (rotate_pairs(rms_scale(queries, query_gain), positions) * query_scale).astype(
        jnp.bfloat16
    )
    keys_new = folded[1].reshape(row_count, heads_here, HD)
    keys_new = (
        rotate_pairs(rms_scale(keys_new, key_gain), positions)
        .astype(jnp.bfloat16)
        .reshape(row_count, kwidth)
    )
    vals_new = folded[2].astype(jnp.bfloat16)
    packed = jnp.concatenate([keys_new, vals_new], axis=1).reshape(micro_count, tok_dev, 2 * kwidth)
    window_rows = window_blocks(packed, tok_dev)
    key_pos = seq_pos[0] - WINDOW + jnp.arange(WINDOW + tok_dev, dtype=jnp.int32)
    mixed_list = []
    for micro_id in range(micro_count):
        block_queries = queries[micro_id * tok_dev : (micro_id + 1) * tok_dev]
        keys_all = window_rows[micro_id, :, :kwidth].reshape(-1, heads_here, HD)
        values_all = window_rows[micro_id, :, kwidth:].reshape(-1, heads_here, HD)
        mixed_list.append(
            window_attention(block_queries, keys_all, values_all, seq_pos, key_pos).reshape(
                tok_dev, qwidth
            )
        )
    mixed_all = jnp.concatenate(mixed_list, axis=0)
    branch = jnp.dot(
        mixed_all, whole_of(w_out, SEQ, (2, 0, 1), 1), preferred_element_type=jnp.float32
    )
    post_full, final_full, head_full = (folded[3], folded[4], folded[5])
    share_width = width // lax.axis_size("section")
    offset = lax.axis_index("section") * share_width
    share = sent_and_summed(branch, "section", 1)
    branch_sq = taken_together(jnp.sum(share * share, axis=1), "section")
    share_scale = lax.rsqrt(branch_sq / width + norm_eps)[:, None]
    post_share = lax.dynamic_slice_in_dim(post_full, offset, share_width, 0)
    updated = (
        lax.dynamic_slice_in_dim(widened, offset, share_width, 1) + share * share_scale * post_share
    ).astype(jnp.bfloat16)
    updated_wide = updated.astype(jnp.float32)
    residual_sq = taken_together(jnp.sum(updated_wide * updated_wide, axis=1), "section")
    final_share = lax.dynamic_slice_in_dim(final_full, offset, share_width, 0)
    last_rows = (
        updated_wide * lax.rsqrt(residual_sq / width + norm_eps)[:, None] * final_share
    ).astype(jnp.bfloat16)
    head_share = lax.dynamic_slice_in_dim(head_full, offset, share_width, 0).astype(jnp.bfloat16)
    raw_values = taken_together(
        jnp.dot(last_rows, head_share, preferred_element_type=jnp.float32), "section"
    )
    raw_values = raw_values.reshape(micro_count, tok_dev)
    token_values = jnp.where(seq_pos[None, :] < lengths[:, None], raw_values, 0.0)
    partial_value = jnp.sum(
        jnp.where(seq_pos[None, :] == reward_pos[:, None], token_values, 0.0), axis=1
    )
    reward = by_axis(partial_value, SEQ)
    return (token_values, reward)


def solution(mesh):
    torus = Mesh(
        mesh.devices.reshape(mesh.shape["section"], 8, 8, 2), ("section", "seq_0", "seq_1", "seq_2")
    )
    in_specs = (
        P(None, SEQ, None),
        P(),
        P(),
        P(SEQ),
        P(SEQ, "section"),
        P(SEQ, "section"),
        P(SEQ, "section"),
        P(),
        P(),
        P("section", SEQ),
        P(SEQ),
        P(SEQ),
        P(SEQ),
    )
    out_specs = (P(None, SEQ), P())
    return jax.shard_map(local, mesh=torus, in_specs=in_specs, out_specs=out_specs, check_vma=False)
```

profile of v0, /device:TPU:2, one launch (start us, length us, event | category | flops | bytes accessed | tf_op | source)
XLA Modules:
  0.0 885.2 jit_solution(14072104166463112967)
XLA Ops:
  11.8 8.6 all-gather
  20.5 28.0 %all_gather.14 = bf16[16,512,21]{1,2,0:T(8,128)(2,1)S(1)} all-gather(bf16[2,512,21]{1,2,0:T(8,128)(2,1)S(1)} %copy.153), channel_id=1, replica_groups=mesh['section'=4,'seq_0'=8,'seq_1'=8,'seq_2'=2] {'seq_0'}, dimensions={0}, use_global_device_ids=true | all-gather | bytes 387072 | tf_op jit(solution)/shard_map/all_gather | solution.py:43
  53.6 558.3 %all-gather.7.cloned.1.call-done = bf16[128,21,1028]{2,1,0:T(8,128)(2,1)} async-done(((bf16[1,21,1028]{2,1,0:T(8,128)(2,1)}), bf16[128,21,1028]{2,1,0:T(8,128)(2,1)}) %all-gather.7.cloned.1.call-update) | async-done | bytes 5526544 | tf_op jit(solution)/shard_map/all_gather | solution.py:29
  611.9 9.2 %reshape.390 = bf16[2688,1028]{1,0:T(8,128)(2,1)} reshape(bf16[128,21,1028]{2,1,0:T(8,128)(2,1)} %all-gather.7.cloned.1.call-done) | data formatting | bytes 11053056
  621.1 3.3 slice_bitcast_fusion.1
  632.2 3.1 fusion.14
  636.0 3.1 collective-permute-start.1
  641.2 17.0 %all-gather.5.cloned.1.call-done = bf16[128,512,21]{1,0,2:T(8,128)(2,1)} async-done(((bf16[16,512,21]{1,0,2:T(8,128)(2,1)}), bf16[128,512,21]{1,0,2:T(8,128)(2,1)}) %all-gather.5.cloned.1.call-update) | async-done | bytes 2752528 | tf_op jit(solution)/shard_map/all_gather | solution.py:43
  658.2 6.5 reshape.382
  664.8 6.4 copy.155
  671.1 5.4 reshape.384
  677.4 2.8 collective-permute-start.2
  680.2 5.0 slice_bitcast_fusion
  686.8 4.5 collective-permute-start
  692.9 4.5 copy.144
  699.1 3.2 multiply_reduce_fusion.2
  702.5 5.0 collective-permute-start.3
  709.5 37.9 %collective-permute-done.3 = bf16[4,2,128,512]{2,3,1,0:T(8,128)(2,1)S(1)} collective-permute-done((bf16[4,2,128,512]{2,3,1,0:T(8,128)(2,1)S(1)}, bf16[4,2,128,512]{2,3,1,0:T(8,128)(2,1)S(1)}, u32[]{:S(2)}, u32[]{:S(2)}) %collective-permute-start.3) | collective-permute-done | bytes 1048608 | tf_op jit(solution)/shard_map/ppermute | solution.py:21
  751.3 3.2 fusion.17
  757.4 3.1 fusion.18
  761.5 4.2 convolution_bitcast_fusion.2
  765.7 4.6 all-to-all-start
  770.3 3.5 fusion.68
  774.0 30.6 %all-to-all-done = f32[4,256,672]{1,2,0:T(8,128)} async-done(((f32[4,256,672]{1,2,0:T(8,128)}), f32[4,256,672]{1,2,0:T(8,128)}, u32[]{:S(2)}, u32[]{:S(2)}) %all-to-all-start) | async-done | bytes 2752544 | tf_op jit(solution)/shard_map/all_to_all | solution.py:61
  807.3 3.2 all-to-all-start.1
  811.7 4.2 all-to-all-done.1
  817.4 3.2 all-to-all-start.2
  821.7 4.2 all-to-all-done.2
  827.2 7.6 all_to_all.23
  835.6 21.5 %psum.21 = f32[2]{0:T(128)S(1)} all-reduce(f32[2]{0:T(128)S(1)} %get-tuple-element.2), channel_id=1, replica_groups=mesh['section'=4,'seq_0'=8,'seq_1'=8,'seq_2'=2] {'seq_0'}, use_global_device_ids=true, to_apply=%region_14.15 | all-reduce | flops 2 | bytes 16 | tf_op jit(solution)/shard_map/psum | solution.py:78
  857.2 15.8 %psum.22 = f32[2]{0:T(128)S(1)} all-reduce(f32[2]{0:T(128)S(1)} %psum.21), channel_id=1, replica_groups=mesh['section'=4,'seq_0'=8,'seq_1'=8,'seq_2'=2] {'seq_1'}, use_global_device_ids=true, to_apply=%region_15.16 | all-reduce | flops 2 | bytes 16 | tf_op jit(solution)/shard_map/psum | solution.py:78
  872.9 5.4 psum.23
  (118 shorter events, 44.2 us)
Async XLA Ops:
  7.2 604.7 %all-gather.7.cloned.1.call-start = ((), (), s32[]{:S(2)}) async-start(), calls=%async_computation.5 | async-start | bytes 7133184 | tf_op jit(solution)/shard_map/all_gather | solution.py:29
  11.8 646.4 %all-gather.5.cloned.1.call-start = ((), (), s32[]{:S(2)}) async-start(), calls=%async_computation.4 | async-start | bytes 3096576 | tf_op jit(solution)/shard_map/all_gather | solution.py:43
  53.6 578.4 %copy-start.8 = (f32[256,64]{0,1:T(8,128)}, f32[256,64]{0,1:T(8,128)S(1)}, u32[]{:S(2)}) copy-start(f32[256,64]{0,1:T(8,128)S(1)} %get-tuple-element.17) | copy-start | bytes 196612
  53.6 578.4 %copy-start.10 = (f32[256,64]{0,1:T(8,128)}, f32[256,64]{0,1:T(8,128)S(1)}, u32[]{:S(2)}) copy-start(f32[256,64]{0,1:T(8,128)S(1)} %get-tuple-element.18) | copy-start | bytes 196612
  627.0 4.3 copy-start.5
  628.5 3.4 copy-start.16
  630.2 1.1 copy-start.4
  632.1 3.2 copy-start.6
  632.2 44.4 %copy-start = (bf16[1,2,128,256]{2,3,1,0:T(8,128)(2,1)}, bf16[1,2,128,256]{2,3,1,0:T(8,128)(2,1)S(1)}, u32[]{:S(2)}) copy-start(bf16[1,2,128,256]{2,3,1,0:T(8,128)(2,1)S(1)} %copy.140) | copy-start | bytes 393220
  635.3 0.7 copy-start.7
  635.9 40.6 %copy-start.2 = (bf16[1,2,128,256]{2,3,1,0:T(8,128)(2,1)}, bf16[1,2,128,256]{2,3,1,0:T(8,128)(2,1)S(1)}, u32[]{:S(2)}) copy-start(bf16[1,2,128,256]{2,3,1,0:T(8,128)(2,1)S(1)} %copy.141) | copy-start | bytes 393220
  635.9 28.8 %copy-start.14 = (bf16[1,2,128,512]{2,3,1,0:T(8,128)(2,1)}, bf16[1,2,128,512]{2,3,1,0:T(8,128)(2,1)S(1)}, u32[]{:S(2)}) copy-start(bf16[1,2,128,512]{2,3,1,0:T(8,128)(2,1)S(1)} %pad_maximum_fusion.2) | copy-start | bytes 786436
  636.0 40.6 %collective-permute-start.1 = (bf16[1,2,128,512]{2,3,1,0:T(8,128)(2,1)S(1)}, bf16[1,2,128,512]{2,3,1,0:T(8,128)(2,1)S(1)}, u32[]{:S(2)}, u32[]{:S(2)}) collective-permute-start(bf16[1,2,128,512]{2,3,1,0:T(8,128)(2,1)S(1)} %pad_maximum_fusion.2), channel_id=1, source_target_pairs={{0,1},{1,2},{2,3},{3,4},{4,5},{5,6},{6,7},{7,8},{8,9},{9,10},{10,1... | collective-permute-start | bytes 786440 | tf_op jit(solution)/shard_map/ppermute | solution.py:21
  677.4 25.0 %collective-permute-start.2 = (bf16[2,2,128,512]{2,3,1,0:T(8,128)(2,1)}, bf16[2,2,128,512]{2,3,1,0:T(8,128)(2,1)S(1)}, u32[]{:S(2)}, u32[]{:S(2)}) collective-permute-start(bf16[2,2,128,512]{2,3,1,0:T(8,128)(2,1)} %pad_maximum_fusion.1), channel_id=1, source_target_pairs={{0,2},{1,3},{2,4},{3,5},{4,6},{5,7},{6,8},{7,9},{8,10},{9,11},{10,... | collective-permute-start | bytes 1572872 | tf_op jit(solution)/shard_map/ppermute | solution.py:21
  686.8 21.7 %collective-permute-start = (bf16[1,2,128,512]{2,3,1,0:T(8,128)(2,1)}, bf16[1,2,128,512]{2,3,1,0:T(8,128)(2,1)}, u32[]{:S(2)}, u32[]{:S(2)}) collective-permute-start(bf16[1,2,128,512]{2,3,1,0:T(8,128)(2,1)} %copy-done.14), channel_id=1, source_target_pairs={{0,8},{1,9},{2,10},{3,11},{4,12},{5,13},{6,14},{7,15},{8,16},{9,17... | collective-permute-start | bytes 786440 | tf_op jit(solution)/shard_map/ppermute | solution.py:21
  699.1 3.2 copy-start.1
  699.1 3.2 copy-start.3
  699.1 8.4 copy-start.17
  702.3 5.3 copy-start.9
  702.3 5.3 copy-start.11
  702.5 44.9 %collective-permute-start.3 = (bf16[4,2,128,512]{2,3,1,0:T(8,128)(2,1)S(1)}, bf16[4,2,128,512]{2,3,1,0:T(8,128)(2,1)S(1)}, u32[]{:S(2)}, u32[]{:S(2)}) collective-permute-start(bf16[4,2,128,512]{2,3,1,0:T(8,128)(2,1)S(1)} %pad_maximum_fusion), channel_id=1, source_target_pairs={{0,4},{1,5},{2,6},{3,7},{4,8},{5,9},{6,10},{7,11},{8,12},{9,13},{1... | collective-permute-start | bytes 3145736 | tf_op jit(solution)/shard_map/ppermute | solution.py:21
  707.8 40.1 %copy-start.12 = (bf16[2,128,256]{1,2,0:T(8,128)(2,1)S(1)}, bf16[2,128,256]{1,2,0:T(8,128)(2,1)}, u32[]{:S(2)}) copy-start(bf16[2,128,256]{1,2,0:T(8,128)(2,1)} %copy.142) | copy-start | bytes 393220
  707.8 40.1 %copy-start.13 = (bf16[2,128,256]{1,2,0:T(8,128)(2,1)S(1)}, bf16[2,128,256]{1,2,0:T(8,128)(2,1)}, u32[]{:S(2)}) copy-start(bf16[2,128,256]{1,2,0:T(8,128)(2,1)} %copy.143) | copy-start | bytes 393220
  748.0 1.3 copy-start.15
  765.7 38.8 %all-to-all-start = ((f32[4,256,672]{1,2,0:T(8,128)}), f32[4,256,672]{1,2,0:T(8,128)}, u32[]{:S(2)}, u32[]{:S(2)}) async-start(f32[4,256,672]{1,2,0:T(8,128)} %convolution_bitcast_fusion.2), calls=%async_computation | async-start | bytes 5505024 | tf_op jit(solution)/shard_map/all_to_all | solution.py:61
  806.6 28.2 %copy-start.18 = (s32[2]{0:T(128)S(1)}, s32[2]{0:T(128)}, u32[]{:S(2)}) copy-start(s32[2]{0:T(128)} %param.15) | copy-start | bytes 28
  806.6 28.2 %copy-start.19 = (s32[2]{0:T(128)S(1)}, s32[2]{0:T(128)}, u32[]{:S(2)}) copy-start(s32[2]{0:T(128)} %param.14) | copy-start | bytes 28
  807.3 8.5 all-to-all-start.1
  817.4 8.5 all-to-all-start.2
Sparse Core Ops, SparseCore 0:
  11.9 599.9 all-gather.6
  614.0 44.1 all-gather.4
where the time goes:
time: 887 us; the launch traced here: 885 us
  waiting for transfers between devices  652 us (74%)
  blocking collectives  87 us (10%)
  local copies, waits for them, and re-layouts  66.1 us (7%)
  starting transfers between devices  26.7 us (3%)
  matrix products  22.5 us (3%)
  other arithmetic  16.2 us (2%)
  between operations  14.6 us (2%)
    all_gather x1, waiting for transfers between devices, sent_together(): whole = lax.all_gather(both, axis, axis=dim, tiled=True)  558 us
    psum x3, blocking collectives, by_axis(): return functools.reduce(lax.psum, axes, array)  42.8 us
    ppermute x4, waiting for transfers between devices, passed_along(): return lax.ppermute(array, axis, pairs)  37.9 us
    all_gather x2, blocking collectives, stacked_from(): tiles = lax.all_gather(tiles, axes[k], axis=0, tiled=True)  36.6 us
    all_to_all x1, waiting for transfers between devices, sent_and_summed(): lax.all_to_all(tiles, axis, split_axis=0, concat_axis=0, tiled=True)  30.6 us
  transfers between devices with their start and end apart: 9, of which 6 were waited for; matrix products, arithmetic and copies ran while one was open for 8% of the time, Pallas kernels for 0%

commit v1 on v0

--- a/solution.py
+++ b/solution.py
@@ -40,7 +40,9 @@
 def stacked_from(array, axes, turns):
     tiles = array[None]
     for k in turns:
-        tiles = lax.all_gather(tiles, axes[k], axis=0, tiled=True)
+        tiles = jnp.concatenate(
+            lax.all_to_all(jnp.stack([tiles] * lax.axis_size(axes[k])), axes[k], 0, 0), axis=0
+        )
     held = [lax.axis_size(axes[k]) for k in reversed(turns)]
     tiles = tiles.reshape(*held, *array.shape)
     turned = sorted(range(len(turns)), key=lambda place: turns[len(turns) - 1 - place])

time: 887 us -> 867 us (0.977)
  blocking collectives: 87 us -> 68.6 us
  waiting for transfers between devices: 652 us -> 637 us
  local copies, waits for them, and re-layouts: 66.1 us -> 75.2 us
    all_gather x2 -> x0, blocking collectives: 36.6 us -> none  [stacked_from(): tiles = lax.all_gather(tiles, axes[k], axis=0, tiled=True)]
    ppermute x4, waiting for transfers between devices: 37.9 us -> 15.8 us  [passed_along(): return lax.ppermute(array, axis, pairs)]
    all_gather x1 -> x0, waiting for transfers between devices: 17 us -> none  [stacked_from(): tiles = lax.all_gather(tiles, axes[k], axis=0, tiled=True)]
    all_to_all x0 -> x2, waiting for transfers between devices: none -> 13 us  [stacked_from(): lax.all_to_all(jnp.stack([tiles] * lax.axis_size(axes[k])), axes[k], 0, 0)]
    all_to_all x0 -> x2, starting transfers between devices: none -> 11.3 us  [stacked_from(): lax.all_to_all(jnp.stack([tiles] * lax.axis_size(axes[k])), axes[k], 0, 0)]
    all_gather x1, waiting for transfers between devices: 558 us -> 569 us  [sent_together(): whole = lax.all_gather(both, axis, axis=dim, tiled=True)]
    all_to_all x0 -> x1, blocking collectives: none -> 10.3 us  [stacked_from(): lax.all_to_all(jnp.stack([tiles] * lax.axis_size(axes[k])), axes[k], 0, 0)]
  transfers between devices with their start and end apart: 9 -> 10, of which waited for: 6 -> 6; matrix products, arithmetic and copies ran while one was open for 8% -> 10% of each run, Pallas kernels for 0% -> 0%
where the time goes in v1:
time: 867 us; the launch traced here: 865 us
  waiting for transfers between devices  637 us (73%)
  local copies, waits for them, and re-layouts  75.2 us (9%)
  blocking collectives  68.6 us (8%)
  starting transfers between devices  30.6 us (4%)
  matrix products  22.5 us (3%)
  other arithmetic  17 us (2%)
  between operations  14.6 us (2%)
    all_gather x1, waiting for transfers between devices, sent_together(): whole = lax.all_gather(both, axis, axis=dim, tiled=True)  569 us
    psum x3, blocking collectives, by_axis(): return functools.reduce(lax.psum, axes, array)  50.7 us
    all_to_all x1, waiting for transfers between devices, sent_and_summed(): lax.all_to_all(tiles, axis, split_axis=0, concat_axis=0, tiled=True)  30.6 us
  transfers between devices with their start and end apart: 10, of which 6 were waited for; matrix products, arithmetic and copies ran while one was open for 10% of the time, Pallas kernels for 0%

profile of v1, /device:TPU:2, one launch (start us, length us, event | category | flops | bytes accessed | tf_op | source)
XLA Modules:
  0.0 865.0 jit_solution(4190547792489884671)
XLA Ops:
  12.6 10.3 %all_to_all.38 = bf16[2,1,512,21]{2,3,1,0:T(8,128)(2,1)S(1)} all-to-all(bf16[2,1,512,21]{2,3,1,0:T(8,128)(2,1)S(1)} %pad_maximum_fusion.3), channel_id=1, replica_groups=mesh['section'=4,'seq_0'=8,'seq_1'=8,'seq_2'=2] {'seq_2'}, dimensions={0} | all-to-all | bytes 86016 | tf_op jit(solution)/shard_map/all_to_all | solution.py:44
  23.8 5.2 all-to-all-start.1
  29.5 13.0 %all-to-all-done.1 = bf16[8,2,512,21]{2,1,3,0:T(2,128)(2,1)S(1)} async-done(((bf16[8,2,512,21]{2,1,3,0:T(2,128)(2,1)}), bf16[8,2,512,21]{2,1,3,0:T(2,128)(2,1)S(1)}, u32[]{:S(2)}, u32[]{:S(2)}) %all-to-all-start.1) | async-done | bytes 344096 | tf_op jit(solution)/shard_map/all_to_all | solution.py:44
  44.9 6.1 all-to-all-start.2
  54.8 568.7 %all-gather.3.cloned.1.call-done = bf16[128,21,1028]{2,1,0:T(8,128)(2,1)} async-done(((bf16[1,21,1028]{2,1,0:T(8,128)(2,1)}), bf16[128,21,1028]{2,1,0:T(8,128)(2,1)}) %all-gather.3.cloned.1.call-update) | async-done | bytes 5526544 | tf_op jit(solution)/shard_map/all_gather | solution.py:29
  623.5 9.2 %reshape.389 = bf16[2688,1028]{1,0:T(8,128)(2,1)} reshape(bf16[128,21,1028]{2,1,0:T(8,128)(2,1)} %all-gather.3.cloned.1.call-done) | data formatting | bytes 11053056
  632.7 3.3 slice_bitcast_fusion.1
  643.8 3.1 fusion.14
  651.8 3.3 copy.185
  655.1 4.4 copy.186
  659.5 6.8 reshape.383
  666.3 5.0 copy.187
  671.3 5.4 reshape.384
  678.8 5.0 slice_bitcast_fusion
  689.0 4.5 copy.174
  695.2 3.2 multiply_reduce_fusion.2
  698.6 2.8 collective-permute-start.3
  703.4 15.8 %collective-permute-done.3 = bf16[4,2,128,512]{2,3,1,0:T(8,128)(2,1)S(1)} collective-permute-done((bf16[4,2,128,512]{2,3,1,0:T(8,128)(2,1)S(1)}, bf16[4,2,128,512]{2,3,1,0:T(8,128)(2,1)S(1)}, u32[]{:S(2)}, u32[]{:S(2)}) %collective-permute-start.3) | collective-permute-done | bytes 1048608 | tf_op jit(solution)/shard_map/ppermute | solution.py:21
  723.1 3.2 fusion.17
  729.2 3.1 fusion.18
  733.3 4.2 convolution_bitcast_fusion.2
  737.5 4.6 all-to-all-start.3
  742.1 3.5 fusion.68
  745.8 30.6 %all-to-all-done.3 = f32[4,256,672]{1,2,0:T(8,128)} async-done(((f32[4,256,672]{1,2,0:T(8,128)}), f32[4,256,672]{1,2,0:T(8,128)}, u32[]{:S(2)}, u32[]{:S(2)}) %all-to-all-start.3) | async-done | bytes 2752544 | tf_op jit(solution)/shard_map/all_to_all | solution.py:63
  779.1 3.2 all-to-all-start.4
  783.5 4.2 all-to-all-done.4
  789.2 3.2 all-to-all-start.5
  793.5 4.2 all-to-all-done.5
  799.0 7.6 all_to_all.39
  807.4 28.0 %psum.21 = f32[2]{0:T(128)S(1)} all-reduce(f32[2]{0:T(128)S(1)} %get-tuple-element.2), channel_id=1, replica_groups=mesh['section'=4,'seq_0'=8,'seq_1'=8,'seq_2'=2] {'seq_0'}, use_global_device_ids=true, to_apply=%region_14.15 | all-reduce | flops 2 | bytes 16 | tf_op jit(solution)/shard_map/psum | solution.py:80
  835.4 17.3 %psum.22 = f32[2]{0:T(128)S(1)} all-reduce(f32[2]{0:T(128)S(1)} %psum.21), channel_id=1, replica_groups=mesh['section'=4,'seq_0'=8,'seq_1'=8,'seq_2'=2] {'seq_1'}, use_global_device_ids=true, to_apply=%region_15.16 | all-reduce | flops 2 | bytes 16 | tf_op jit(solution)/shard_map/psum | solution.py:80
  852.7 5.4 psum.23
  (123 shorter events, 52.8 us)
Async XLA Ops:
  7.2 616.3 %all-gather.3.cloned.1.call-start = ((), (), s32[]{:S(2)}) async-start(), calls=%async_computation.7 | async-start | bytes 7133184 | tf_op jit(solution)/shard_map/all_gather | solution.py:29
  23.8 18.7 %all-to-all-start.1 = ((bf16[8,2,512,21]{2,1,3,0:T(2,128)(2,1)}), bf16[8,2,512,21]{2,1,3,0:T(2,128)(2,1)S(1)}, u32[]{:S(2)}, u32[]{:S(2)}) async-start(bf16[8,2,512,21]{2,1,3,0:T(2,128)(2,1)} %stack.19), calls=%async_computation.1 | async-start | bytes 688128 | tf_op jit(solution)/shard_map/all_to_all | solution.py:44
  44.9 606.9 %all-to-all-start.2 = ((bf16[8,16,512,21]{2,1,3,0:T(8,128)(2,1)}), bf16[8,16,512,21]{2,1,3,0:T(8,128)(2,1)}, u32[]{:S(2)}, u32[]{:S(2)}) async-start(bf16[8,16,512,21]{2,1,3,0:T(8,128)(2,1)} %stack.20), calls=%async_computation.2 | async-start | bytes 5505024 | tf_op jit(solution)/shard_map/all_to_all | solution.py:44
  54.7 588.8 %copy-start.8 = (f32[256,64]{0,1:T(8,128)}, f32[256,64]{0,1:T(8,128)S(1)}, u32[]{:S(2)}) copy-start(f32[256,64]{0,1:T(8,128)S(1)} %get-tuple-element.17) | copy-start | bytes 196612
  54.8 588.8 %copy-start.10 = (f32[256,64]{0,1:T(8,128)}, f32[256,64]{0,1:T(8,128)S(1)}, u32[]{:S(2)}) copy-start(f32[256,64]{0,1:T(8,128)S(1)} %get-tuple-element.18) | copy-start | bytes 196612
  638.6 4.3 copy-start.5
  640.0 3.4 copy-start.16
  641.8 1.1 copy-start.4
  643.7 3.2 copy-start.6
  643.7 32.9 %copy-start = (bf16[1,2,128,256]{2,3,1,0:T(8,128)(2,1)}, bf16[1,2,128,256]{2,3,1,0:T(8,128)(2,1)S(1)}, u32[]{:S(2)}) copy-start(bf16[1,2,128,256]{2,3,1,0:T(8,128)(2,1)S(1)} %copy.170) | copy-start | bytes 393220
  646.8 0.7 copy-start.7
  647.5 29.2 %copy-start.2 = (bf16[1,2,128,256]{2,3,1,0:T(8,128)(2,1)}, bf16[1,2,128,256]{2,3,1,0:T(8,128)(2,1)S(1)}, u32[]{:S(2)}) copy-start(bf16[1,2,128,256]{2,3,1,0:T(8,128)(2,1)S(1)} %copy.171) | copy-start | bytes 393220
  647.5 7.6 copy-start.14
  647.5 29.2 %collective-permute-start.1 = (bf16[1,2,128,512]{2,3,1,0:T(8,128)(2,1)S(1)}, bf16[1,2,128,512]{2,3,1,0:T(8,128)(2,1)S(1)}, u32[]{:S(2)}, u32[]{:S(2)}) collective-permute-start(bf16[1,2,128,512]{2,3,1,0:T(8,128)(2,1)S(1)} %pad_maximum_fusion.2), channel_id=1, source_target_pairs={{0,1},{1,2},{2,3},{3,4},{4,5},{5,6},{6,7},{7,8},{8,9},{9,10},{10,1... | collective-permute-start | bytes 786440 | tf_op jit(solution)/shard_map/ppermute | solution.py:21
  677.5 20.9 %collective-permute-start.2 = (bf16[2,2,128,512]{2,3,1,0:T(8,128)(2,1)}, bf16[2,2,128,512]{2,3,1,0:T(8,128)(2,1)S(1)}, u32[]{:S(2)}, u32[]{:S(2)}) collective-permute-start(bf16[2,2,128,512]{2,3,1,0:T(8,128)(2,1)} %pad_maximum_fusion.1), channel_id=1, source_target_pairs={{0,2},{1,3},{2,4},{3,5},{4,6},{5,7},{6,8},{7,9},{8,10},{9,11},{10,... | collective-permute-start | bytes 1572872 | tf_op jit(solution)/shard_map/ppermute | solution.py:21
  685.5 16.9 %collective-permute-start = (bf16[1,2,128,512]{2,3,1,0:T(8,128)(2,1)}, bf16[1,2,128,512]{2,3,1,0:T(8,128)(2,1)}, u32[]{:S(2)}, u32[]{:S(2)}) collective-permute-start(bf16[1,2,128,512]{2,3,1,0:T(8,128)(2,1)} %copy-done.14), channel_id=1, source_target_pairs={{0,8},{1,9},{2,10},{3,11},{4,12},{5,13},{6,14},{7,15},{8,16},{9,17... | collective-permute-start | bytes 786440 | tf_op jit(solution)/shard_map/ppermute | solution.py:21
  695.2 3.2 copy-start.1
  695.2 3.2 copy-start.3
  695.2 6.2 copy-start.17
  698.4 3.1 copy-start.9
  698.4 3.1 copy-start.11
  698.6 20.6 %collective-permute-start.3 = (bf16[4,2,128,512]{2,3,1,0:T(8,128)(2,1)S(1)}, bf16[4,2,128,512]{2,3,1,0:T(8,128)(2,1)S(1)}, u32[]{:S(2)}, u32[]{:S(2)}) collective-permute-start(bf16[4,2,128,512]{2,3,1,0:T(8,128)(2,1)S(1)} %pad_maximum_fusion), channel_id=1, source_target_pairs={{0,4},{1,5},{2,6},{3,7},{4,8},{5,9},{6,10},{7,11},{8,12},{9,13},{1... | collective-permute-start | bytes 3145736 | tf_op jit(solution)/shard_map/ppermute | solution.py:21
  701.6 18.1 %copy-start.12 = (bf16[2,128,256]{1,2,0:T(8,128)(2,1)S(1)}, bf16[2,128,256]{1,2,0:T(8,128)(2,1)}, u32[]{:S(2)}) copy-start(bf16[2,128,256]{1,2,0:T(8,128)(2,1)} %copy.172) | copy-start | bytes 393220
  701.6 18.1 %copy-start.13 = (bf16[2,128,256]{1,2,0:T(8,128)(2,1)S(1)}, bf16[2,128,256]{1,2,0:T(8,128)(2,1)}, u32[]{:S(2)}) copy-start(bf16[2,128,256]{1,2,0:T(8,128)(2,1)} %copy.173) | copy-start | bytes 393220
  719.8 1.3 copy-start.15
  737.5 38.8 %all-to-all-start.3 = ((f32[4,256,672]{1,2,0:T(8,128)}), f32[4,256,672]{1,2,0:T(8,128)}, u32[]{:S(2)}, u32[]{:S(2)}) async-start(f32[4,256,672]{1,2,0:T(8,128)} %convolution_bitcast_fusion.2), calls=%async_computation.3 | async-start | bytes 5505024 | tf_op jit(solution)/shard_map/all_to_all | solution.py:63
  778.4 28.2 %copy-start.18 = (s32[2]{0:T(128)S(1)}, s32[2]{0:T(128)}, u32[]{:S(2)}) copy-start(s32[2]{0:T(128)} %param.15) | copy-start | bytes 28
  778.4 28.2 %copy-start.19 = (s32[2]{0:T(128)S(1)}, s32[2]{0:T(128)}, u32[]{:S(2)}) copy-start(s32[2]{0:T(128)} %param.14) | copy-start | bytes 28
  779.1 8.5 all-to-all-start.4
  789.2 8.5 all-to-all-start.5
Sparse Core Ops, SparseCore 0:
  11.9 611.5 all-gather.2
